TPU v7x, 32 devices: a whole 2x2x4 slice. The times are simulated.
32 devices in a mesh: groups: 2 (over y), pair: 4 (over z), vir: 2 (over x), sub: 2 (over core).
Axes of the slice: x: 2, y: 2, z: 4, core: 2. Of those that a mesh axis runs over, the one named last changes fastest.
Arguments:
- amplitudes: bfloat16 [8, 36, 128, 128], P(('groups', 'pair'), 'vir', 'sub'), parts along dimension 0, may hold values from -1 to 1
- pair_list: int32 [8, 2], P(('groups', 'pair')), parts along dimension 0, may hold values from 0 to 255, as said below
- tile_list: int32 [36, 2], replicated, may hold values from 0 to 7, as said below
Outputs:
- p_virt: float32 [72, 128, 128], P(('groups', 'vir'), 'sub'), parts along dimension 0
- p_occ: float32 [512, 256], P('groups'), parts along dimension 0
There are 2 independent parts, one for each index of `groups`. A program takes and returns all parts, laid end to end along the dimension named above; an argument that names none is the same for every part. Nothing has to cross between parts.
Inputs may be any that keep to these rules, and one draw needn't show every extreme that they name: `pair_list`: each row holds two different occupied orbitals in increasing order; no two rows are equal. `tile_list`: each row holds a tile row and a tile column, row <= column; every such couple of the 8 x 8 tile grid appears exactly once.
All inputs are finite; a program needn't handle non-finite values.
Results may differ from a plain program's by a relative error of at most 0.0003.
Values may be sent and summed in bfloat16 or wider, within the bound.
A program may use at most 64 MiB of HBM per device.

v0:
```python
import jax
import jax.numpy as jnp
from jax import lax
from jax.sharding import PartitionSpec as P

OCC = 256
NTV = 8
NT = 36


def from_behind(array, axis, by):
    peers = lax.axis_size(axis)
    return lax.ppermute(array, axis, [(i, (i + by) % peers) for i in range(peers)])


def slot_table(tile_list):
    tile_grid = jnp.arange(NTV, dtype=jnp.int32)
    upper_hit = (tile_list[:, 0][None, None, :] == tile_grid[:, None, None]) & (
        tile_list[:, 1][None, None, :] == tile_grid[None, :, None]
    )
    either_hit = upper_hit | jnp.transpose(upper_hit, (1, 0, 2))
    slot_ids = jnp.arange(NT, dtype=jnp.int32)
    return jnp.sum(jnp.where(either_hit, slot_ids[None, None, :], 0), axis=2)


def occurrences(pair_rows):
    orbital = jnp.concatenate([pair_rows[:, 0], pair_rows[:, 1]])
    partner = jnp.concatenate([pair_rows[:, 1], pair_rows[:, 0]])
    pair_count = pair_rows.shape[0]
    parity = jnp.concatenate(
        [jnp.ones((pair_count,), jnp.float32), -jnp.ones((pair_count,), jnp.float32)]
    )
    return (orbital, partner, parity)


def occ_density(pair_gram, left_pairs, right_pairs):
    left_orb, left_partner, left_sign = occurrences(left_pairs)
    right_orb, right_partner, right_sign = occurrences(right_pairs)
    doubled = jnp.tile(pair_gram, (2, 2))
    couple = jnp.where(
        left_partner[:, None] == right_partner[None, :],
        left_sign[:, None] * right_sign[None, :] * doubled,
        0.0,
    )
    orbitals = jnp.arange(OCC, dtype=jnp.int32)
    left_hot = (left_orb[:, None] == orbitals[None, :]).astype(jnp.float32)
    right_hot = (right_orb[:, None] == orbitals[None, :]).astype(jnp.float32)
    inner_sum = jnp.dot(couple, right_hot, precision=lax.Precision.HIGHEST)
    return -jnp.dot(left_hot.T, inner_sum, precision=lax.Precision.HIGHEST)


def share_gram(masked, visiting):
    left_flat = masked.reshape(masked.shape[0], -1)
    right_flat = visiting.reshape(visiting.shape[0], -1)
    return lax.dot_general(
        left_flat, right_flat, (((1,), (1,)), ((), ())), preferred_element_type=jnp.float32
    )


def oriented(packed, slot_grid, tile_ids, column):
    gathered = packed[:, slot_grid[tile_ids, column]]
    turned = jnp.swapaxes(gathered, 2, 3)
    on_or_above = (tile_ids <= column)[None, :, None, None]
    on_or_below = (tile_ids >= column)[None, :, None, None]
    nothing = jnp.zeros_like(gathered)
    return jnp.where(on_or_above, gathered, nothing) - jnp.where(on_or_below, turned, nothing)


def shards(amplitudes, pair_list, tile_list):
    pair_dev, slot_dev, row_dev, tile_width = amplitudes.shape
    n_pair = lax.axis_size("pair")
    pair_at = lax.axis_index("pair")
    vir_at = lax.axis_index("vir")
    sub_at = lax.axis_index("sub")
    nothing = jnp.zeros((), jnp.bfloat16)
    in_tile = jnp.arange(tile_width, dtype=jnp.int32)
    own_list = lax.dynamic_slice_in_dim(tile_list, vir_at * slot_dev, slot_dev, 0)
    own_rows = sub_at * row_dev + jnp.arange(row_dev, dtype=jnp.int32)
    own_diagonal = own_list[:, 0] == own_list[:, 1]
    own_lower = in_tile[None, :] <= own_rows[:, None]
    own_keep = jnp.logical_not(own_diagonal[:, None, None] & own_lower[None])
    masked = jnp.where(own_keep[None], amplitudes, nothing)
    all_pairs = lax.all_gather(pair_list, "pair", axis=0, tiled=True)

    def anchor_of(distance):
        return (pair_at - distance) % n_pair

    def place(rows, block, distance):
        column_at = anchor_of(distance) * pair_dev
        return lax.dynamic_update_slice(rows, block, (jnp.zeros((), jnp.int32), column_at))

    def fold(running, block, distance):
        both_rows, half_rows = running
        return (place(both_rows, block, distance), half_rows)

    rows_zero = jnp.zeros((pair_dev, n_pair * pair_dev), jnp.float32)
    start = (rows_zero, rows_zero)
    running = fold(start, share_gram(masked, amplitudes), 0)

    def full_turn(turn_index, state_pair):
        visiting, carried = state_pair
        visiting = from_behind(visiting, "pair", 1)
        carried = fold(carried, share_gram(masked, visiting), turn_index + 1)
        return (visiting, carried)

    _, running = lax.fori_loop(0, n_pair - 1, full_turn, (amplitudes, running))
    summed = lax.psum((running[0], running[1]), ("vir", "sub"))
    both_whole, half_whole = (
        lax.all_gather(summed[0], "pair", axis=0, tiled=True),
        lax.all_gather(summed[1], "pair", axis=0, tiled=True),
    )
    full_gram = both_whole + half_whole + half_whole.T
    p_occ = occ_density(full_gram, all_pairs, all_pairs)
    rows_whole = lax.all_gather(amplitudes, "sub", axis=2, tiled=True)
    packed = lax.all_gather(rows_whole, "vir", axis=1, tiled=True)
    all_diagonal = tile_list[:, 0] == tile_list[:, 1]
    all_lower = in_tile[None, :] <= in_tile[:, None]
    all_keep = jnp.logical_not(all_diagonal[:, None, None] & all_lower[None])
    packed = jnp.where(all_keep[None], packed, nothing)
    slot_grid = slot_table(tile_list)
    left_ids = own_list[:, 0]
    right_ids = own_list[:, 1]
    virt_part = jnp.zeros((slot_dev, row_dev, tile_width), jnp.float32)
    for column in range(NTV):
        left_block = oriented(packed, slot_grid, left_ids, column)
        left_block = lax.dynamic_slice_in_dim(left_block, sub_at * row_dev, row_dev, 2)
        right_block = oriented(packed, slot_grid, right_ids, column)
        virt_part = virt_part + jnp.einsum(
            "psxz,psyz->sxy", left_block, right_block, preferred_element_type=jnp.float32
        )
    p_virt = lax.psum(virt_part, "pair")
    return (p_virt, p_occ)


def solution(mesh):
    in_specs = (P(("groups", "pair"), "vir", "sub", None), P(("groups", "pair"), None), P())
    out_specs = (P(("groups", "vir"), "sub", None), P("groups", None))
    return jax.shard_map(shards, mesh=mesh, in_specs=in_specs, out_specs=out_specs, check_vma=False)
```

profile of v0, /device:TPU:0, one launch (start us, length us, event | category | flops | bytes accessed | tf_op | source)
XLA Modules:
  0.0 147.8 jit_solution(3376896887680750675)
XLA Ops:
  7.2 1.0 copy.166
  8.2 2.5 %all_gather.13 = bf16[1,18,128,128]{3,2,0,1:T(8,128)(2,1)} all-gather(bf16[1,18,64,128]{3,2,0,1:T(8,128)(2,1)S(1)} %bitcast.348), channel_id=1, replica_groups=mesh['groups'=2,'pair'=4,'vir'=2,'sub'=2] {'sub'}, dimensions={2}, use_global_device_ids=true | all-gather | bytes 884736 | tf_op jit(solution)/shard_map/all_gather | solution.py:114
  11.7 0.7 gather_fusion
  12.5 0.7 gather_fusion.2
  13.2 0.7 gather_fusion.4
  14.0 0.7 gather_fusion.6
  14.8 0.7 gather_fusion.8
  15.5 0.7 gather_fusion.10
  16.3 0.7 gather_fusion.12
  17.0 0.7 gather_fusion.14
  17.8 0.7 gather_fusion.16
  18.6 0.7 gather_fusion.18
  19.3 0.7 gather_fusion.20
  20.1 0.7 gather_fusion.22
  20.9 0.7 gather_fusion.24
  21.6 0.7 gather_fusion.26
  22.4 0.7 gather_fusion.28
  23.1 0.7 gather_fusion.30
  24.0 0.9 fusion.2
  24.9 12.5 %all-gather = s32[4,1,2]{2,1,0:T(1,128)S(1)} all-gather(s32[1,1,2]{2,1,0:T(1,128)S(1)} %bitcast.377), channel_id=1, replica_groups=mesh['groups'=2,'pair'=4,'vir'=2,'sub'=2] {'pair'}, dimensions={0}, use_global_device_ids=true | all-gather | bytes 40 | tf_op jit(solution)/shard_map/all_gather | solution.py:83
  37.5 0.9 dynamic_update_slice.13
  39.9 1.7 %fusion.1 = bf16[36,128,128]{2,1,0:T(8,128)(2,1)S(1)} fusion(bf16[1,36,128,128]{3,2,0,1:T(8,128)(2,1)} %all-gather.4.cloned.1.call-done, pred[128,128]{1,0:T(8,128)(4,1)S(1)} %iota_compare_fusion, pred[36]{0:T(512)(128)(4,1)S(1)} %fusion.149), kind=kLoop, calls=%fused_computation.42 | loop fusion | flops 1179648 | bytes 2375716 | tf_op jit(solution)/shard_map/jit(_where)/select_n | solution.py:119
  41.6 0.7 gather_fusion.1
  42.3 1.1 copy.110
  43.4 0.7 gather_fusion.3
  44.1 1.1 copy.112
  45.2 0.7 gather_fusion.5
  45.9 1.1 copy.114
  47.6 1.1 copy.116
  48.7 0.7 gather_fusion.9
  49.4 1.1 copy.118
  51.1 1.1 copy.120
  52.2 0.7 gather_fusion.13
  52.9 1.1 copy.122
  54.7 1.1 copy.124
  56.4 1.1 copy.126
  57.5 0.7 gather_fusion.19
  58.2 1.1 copy.128
  60.0 1.1 copy.130
  61.8 1.1 copy.132
  63.5 1.1 copy.134
  65.3 0.8 copy-done
  66.1 1.1 copy.136
  67.8 1.1 copy.138
  69.6 1.1 copy.139
  70.7 0.8 select_bitcast_fusion.7
  72.0 0.7 copy-done.29
  73.1 0.7 copy-done.31
  74.2 0.7 copy-done.33
  85.0 1.2 convolution_add_fusion
  86.3 37.7 %while.17 = (s32[]{:T(128)}, bf16[1,18,64,128]{3,2,1,0:T(8,128)(2,1)S(1)}, f32[1,4]{1,0:T(1,128)S(1)}, bf16[1,18,64,128]{3,2,1,0:T(8,128)(2,1)S(1)}, s32[]{:T(12...) while((s32[]{:T(128)}, bf16[1,18,64,128]{3,2,1,0:T(8,128)(2,1)S(1)}, f32[1,4]{1,0:T(1,128)S(1)}, ...), condition=%wide.region_3.4_spmd, body=%wide.region_2.3_spmd.sunk | while | flops 589840 | bytes 2359600 | solution.py:106
  86.4 11.4 %collective-permute-done = bf16[1,18,64,128]{3,2,1,0:T(8,128)(2,1)S(1)} collective-permute-done((bf16[1,18,64,128]{3,2,1,0:T(8,128)(2,1)S(1)}, bf16[1,18,64,128]{3,2,1,0:T(8,128)(2,1)S(1)}, u32[]{:S(2)}, u32[]{:S(2)}) %collective-permute-start) | collective-permute-done | bytes 294944 | tf_op jit(solution)/shard_map/while/body/eval_jaxpr/ppermute | solution.py:13
  97.8 0.8 fusion.154
  98.5 0.8 dynamic_update_slice.15
  99.4 11.6 %collective-permute-done = bf16[1,18,64,128]{3,2,1,0:T(8,128)(2,1)S(1)} collective-permute-done((bf16[1,18,64,128]{3,2,1,0:T(8,128)(2,1)S(1)}, bf16[1,18,64,128]{3,2,1,0:T(8,128)(2,1)S(1)}, u32[]{:S(2)}, u32[]{:S(2)}) %collective-permute-start) | collective-permute-done | bytes 294944 | tf_op jit(solution)/shard_map/while/body/eval_jaxpr/ppermute | solution.py:13
  111.0 0.8 fusion.154
  111.8 0.8 dynamic_update_slice.15
  112.6 9.8 %collective-permute-done = bf16[1,18,64,128]{3,2,1,0:T(8,128)(2,1)S(1)} collective-permute-done((bf16[1,18,64,128]{3,2,1,0:T(8,128)(2,1)S(1)}, bf16[1,18,64,128]{3,2,1,0:T(8,128)(2,1)S(1)}, u32[]{:S(2)}, u32[]{:S(2)}) %collective-permute-start) | collective-permute-done | bytes 294944 | tf_op jit(solution)/shard_map/while/body/eval_jaxpr/ppermute | solution.py:13
  122.4 0.8 fusion.154
  123.2 0.8 dynamic_update_slice.15
  124.0 6.1 %psum.18 = f32[1,4]{1,0:T(1,128)S(1)} all-reduce(f32[1,4]{1,0:T(1,128)S(1)} %get-tuple-element.135), channel_id=1, replica_groups=mesh['groups'=2,'pair'=4,'vir'=2,'sub'=2] {'vir','sub'}, use_global_device_ids=true, to_apply=%region_4.5 | all-reduce | flops 4 | bytes 32 | tf_op jit(solution)/shard_map/psum | solution.py:107
  130.0 7.6 %all-gather.1 = f32[4,1,4]{2,1,0:T(1,128)S(1)} all-gather(f32[1,1,4]{2,1,0:T(1,128)S(1)} %bitcast.378), channel_id=1, replica_groups=mesh['groups'=2,'pair'=4,'vir'=2,'sub'=2] {'pair'}, dimensions={0}, use_global_device_ids=true | all-gather | bytes 80 | tf_op jit(solution)/shard_map/all_gather | solution.py:109
  138.0 1.1 convolution_negate_fusion
  139.1 1.9 %copy.167 = f32[18,64,128]{2,1,0:T(8,128)} copy(f32[18,64,128]{2,1,0:T(8,128)} %all-reduce.18.cloned.1.call-done) | data formatting | bytes 1179648
  (238 shorter events, 21.2 us)
Async XLA Ops:
  7.2 3.6 %copy-start.42 = (s32[36,2]{0,1:T(2,128)S(1)}, s32[36,2]{0,1:T(2,128)}, u32[]{:S(2)}) copy-start(s32[36,2]{0,1:T(2,128)} %param.7) | copy-start | bytes 868
  7.2 32.7 %all-gather.4.cloned.1.call-start = ((), (), s32[]{:S(2)}) async-start(), calls=%async_computation | async-start | bytes 1769472 | tf_op jit(solution)/shard_map/all_gather | solution.py:115
  10.7 128.4 %all-reduce.18.cloned.1.call-start = ((), (), s32[]{:S(2)}) async-start(), calls=%async_computation.1 | async-start | bytes 1179648 | tf_op jit(solution)/shard_map/psum | solution.py:131
  20.8 4.1 %copy-start.49 = (s32[1,2]{1,0:T(1,128)S(1)}, s32[1,2]{1,0:T(1,128)}, u32[]{:S(2)}) copy-start(s32[1,2]{1,0:T(1,128)} %param.6) | copy-start | bytes 28
  42.3 1.8 %copy-start.20 = (bf16[18,128,128]{2,1,0:T(8,128)(2,1)}, bf16[18,128,128]{2,1,0:T(8,128)(2,1)S(1)}, u32[]{:S(2)}) copy-start(bf16[18,128,128]{2,1,0:T(8,128)(2,1)S(1)} %gather_fusion.1) | copy-start | bytes 1769476
  44.1 1.7 %copy-start.24 = (bf16[18,128,128]{2,1,0:T(8,128)(2,1)}, bf16[18,128,128]{2,1,0:T(8,128)(2,1)S(1)}, u32[]{:S(2)}) copy-start(bf16[18,128,128]{2,1,0:T(8,128)(2,1)S(1)} %gather_fusion.3) | copy-start | bytes 1769476
  45.9 1.7 %copy-start.18 = (bf16[18,128,128]{2,1,0:T(8,128)(2,1)}, bf16[18,128,128]{2,1,0:T(8,128)(2,1)S(1)}, u32[]{:S(2)}) copy-start(bf16[18,128,128]{2,1,0:T(8,128)(2,1)S(1)} %gather_fusion.5) | copy-start | bytes 1769476
  47.6 1.8 %copy-start.22 = (bf16[18,128,128]{2,1,0:T(8,128)(2,1)}, bf16[18,128,128]{2,1,0:T(8,128)(2,1)S(1)}, u32[]{:S(2)}) copy-start(bf16[18,128,128]{2,1,0:T(8,128)(2,1)S(1)} %gather_fusion.7) | copy-start | bytes 1769476
  49.4 1.7 %copy-start.14 = (bf16[18,128,128]{2,1,0:T(8,128)(2,1)}, bf16[18,128,128]{2,1,0:T(8,128)(2,1)S(1)}, u32[]{:S(2)}) copy-start(bf16[18,128,128]{2,1,0:T(8,128)(2,1)S(1)} %gather_fusion.9) | copy-start | bytes 1769476
  51.1 1.8 %copy-start.16 = (bf16[18,128,128]{2,1,0:T(8,128)(2,1)}, bf16[18,128,128]{2,1,0:T(8,128)(2,1)S(1)}, u32[]{:S(2)}) copy-start(bf16[18,128,128]{2,1,0:T(8,128)(2,1)S(1)} %gather_fusion.11) | copy-start | bytes 1769476
  52.9 1.7 %copy-start.10 = (bf16[18,128,128]{2,1,0:T(8,128)(2,1)}, bf16[18,128,128]{2,1,0:T(8,128)(2,1)S(1)}, u32[]{:S(2)}) copy-start(bf16[18,128,128]{2,1,0:T(8,128)(2,1)S(1)} %gather_fusion.13) | copy-start | bytes 1769476
  54.7 1.7 %copy-start.12 = (bf16[18,128,128]{2,1,0:T(8,128)(2,1)}, bf16[18,128,128]{2,1,0:T(8,128)(2,1)S(1)}, u32[]{:S(2)}) copy-start(bf16[18,128,128]{2,1,0:T(8,128)(2,1)S(1)} %gather_fusion.15) | copy-start | bytes 1769476
  56.4 1.8 %copy-start.6 = (bf16[18,128,128]{2,1,0:T(8,128)(2,1)}, bf16[18,128,128]{2,1,0:T(8,128)(2,1)S(1)}, u32[]{:S(2)}) copy-start(bf16[18,128,128]{2,1,0:T(8,128)(2,1)S(1)} %gather_fusion.17) | copy-start | bytes 1769476
  58.2 1.8 %copy-start.8 = (bf16[18,128,128]{2,1,0:T(8,128)(2,1)}, bf16[18,128,128]{2,1,0:T(8,128)(2,1)S(1)}, u32[]{:S(2)}) copy-start(bf16[18,128,128]{2,1,0:T(8,128)(2,1)S(1)} %gather_fusion.19) | copy-start | bytes 1769476
  60.0 1.8 %copy-start.2 = (bf16[18,128,128]{2,1,0:T(8,128)(2,1)}, bf16[18,128,128]{2,1,0:T(8,128)(2,1)S(1)}, u32[]{:S(2)}) copy-start(bf16[18,128,128]{2,1,0:T(8,128)(2,1)S(1)} %gather_fusion.21) | copy-start | bytes 1769476
  61.8 1.7 %copy-start.4 = (bf16[18,128,128]{2,1,0:T(8,128)(2,1)}, bf16[18,128,128]{2,1,0:T(8,128)(2,1)S(1)}, u32[]{:S(2)}) copy-start(bf16[18,128,128]{2,1,0:T(8,128)(2,1)S(1)} %gather_fusion.23) | copy-start | bytes 1769476
  69.6 1.1 copy-start.26
  69.6 1.9 %copy-start.27 = (bf16[1,18,128,128]{2,3,1,0:T(8,128)(2,1)S(1)}, bf16[1,18,128,128]{2,3,1,0:T(8,128)(2,1)}, u32[]{:S(2)}) copy-start(bf16[1,18,128,128]{2,3,1,0:T(8,128)(2,1)} %copy.114) | copy-start | bytes 1769476
  70.7 1.1 copy-start.28
  70.7 1.1 copy-start.45
  71.6 1.1 copy-start.29
  71.8 1.1 copy-start.30
  71.8 1.1 copy-start.43
  74.1 1.3 copy-start.25
  74.1 1.5 copy-start.41
  74.1 1.5 copy-start.71
  74.1 1.5 copy-start.72
  74.1 1.4 copy-start.73
  75.5 1.2 copy-start.23
  75.6 1.4 copy-start.40
  75.6 1.4 copy-start.57
  75.6 1.4 copy-start.69
  75.6 1.4 copy-start.70
  77.0 1.2 copy-start.17
  77.0 1.4 copy-start.39
  77.0 1.4 copy-start.56
  77.0 1.4 copy-start.67
  77.0 1.4 copy-start.68
  78.4 1.2 copy-start.13
  78.4 1.4 copy-start.38
  78.4 1.4 copy-start.55
  78.4 1.4 copy-start.65
  78.4 1.4 copy-start.66
  79.8 1.2 copy-start.9
  79.8 1.4 copy-start.37
  79.9 1.4 copy-start.54
  79.9 1.4 copy-start.63
  79.9 1.4 copy-start.64
  81.3 1.2 copy-start.5
  81.3 1.4 copy-start.36
  81.3 1.4 copy-start.53
  81.3 1.4 copy-start.61
  81.3 1.4 copy-start.62
  82.7 1.2 copy-start.35
  82.7 1.2 copy-start.52
  82.7 1.2 copy-start.59
  82.7 1.2 copy-start.60
  85.0 1.2 copy-start.75
  86.3 51.4 %copy-start.47 = (s32[4]{0:T(128)S(1)}, s32[4]{0:T(128)}, u32[]{:S(2)}) copy-start(s32[4]{0:T(128)} %get-tuple-element.152) | copy-start | bytes 52
  86.3 51.4 %copy-start.48 = (s32[4]{0:T(128)S(1)}, s32[4]{0:T(128)}, u32[]{:S(2)}) copy-start(s32[4]{0:T(128)} %get-tuple-element.153) | copy-start | bytes 52
  86.3 51.5 %copy-start.76 = (f32[8]{0:T(128)S(1)}, f32[8]{0:T(128)}, u32[]{:S(2)}) copy-start(f32[8]{0:T(128)} %constant.110.clone.1) | copy-start | bytes 100
  86.3 11.5 %collective-permute-start = (bf16[1,18,64,128]{3,2,1,0:T(8,128)(2,1)S(1)}, bf16[1,18,64,128]{3,2,1,0:T(8,128)(2,1)S(1)}, u32[]{:S(2)}, u32[]{:S(2)}) collective-permute-start(bf16[1,18,64,128]{3,2,1,0:T(8,128)(2,1)S(1)} %get-tuple-element.252), channel_id=1, source_target_pairs={{0,4},{4,8},{8,12},{12,0},{1,5},{5,9},{9,13},{13,1},{2,6},{6,10},{... | collective-permute-start | bytes 884744 | tf_op jit(solution)/shard_map/while/body/eval_jaxpr/ppermute | solution.py:13
  99.3 11.7 %collective-permute-start = (bf16[1,18,64,128]{3,2,1,0:T(8,128)(2,1)S(1)}, bf16[1,18,64,128]{3,2,1,0:T(8,128)(2,1)S(1)}, u32[]{:S(2)}, u32[]{:S(2)}) collective-permute-start(bf16[1,18,64,128]{3,2,1,0:T(8,128)(2,1)S(1)} %get-tuple-element.252), channel_id=1, source_target_pairs={{0,4},{4,8},{8,12},{12,0},{1,5},{5,9},{9,13},{13,1},{2,6},{6,10},{... | collective-permute-start | bytes 884744 | tf_op jit(solution)/shard_map/while/body/eval_jaxpr/ppermute | solution.py:13
  112.5 9.9 %collective-permute-start = (bf16[1,18,64,128]{3,2,1,0:T(8,128)(2,1)S(1)}, bf16[1,18,64,128]{3,2,1,0:T(8,128)(2,1)S(1)}, u32[]{:S(2)}, u32[]{:S(2)}) collective-permute-start(bf16[1,18,64,128]{3,2,1,0:T(8,128)(2,1)S(1)} %get-tuple-element.252), channel_id=1, source_target_pairs={{0,4},{4,8},{8,12},{12,0},{1,5},{5,9},{9,13},{13,1},{2,6},{6,10},{... | collective-permute-start | bytes 884744 | tf_op jit(solution)/shard_map/while/body/eval_jaxpr/ppermute | solution.py:13
  (18 other events, 18.5 us)
Sparse Core Ops, SparseCore 0:
  10.8 25.3 all-gather.3
  86.4 45.5 all-reduce.17
where the time goes:
time: 148 us
  local copies, waits for them, and re-layouts  55.8 us (38%)
  waiting for transfers between devices  32.8 us (22%)
  blocking collectives  28.6 us (19%)
  between operations  15 us (10%)
  other arithmetic  8.57 us (6%)
  matrix products  6.62 us (4%)
    gather x48, local copies, waits for them, and re-layouts, oriented(): gathered = packed[:, slot_grid[tile_ids, column]]  39.8 us
    ppermute x3, waiting for transfers between devices, from_behind(): lax.ppermute(array, axis, [(i, (i + by) % peers) for i in range(peers)])  32.8 us
    all_gather x1, blocking collectives, shards(): all_pairs = lax.all_gather(pair_list, 'pair', axis=0, tiled=True)  12.5 us
    unnamed x156, local copies, waits for them, and re-layouts  12 us
    all_gather x1, blocking collectives, shards(): lax.all_gather(summed[0], 'pair', axis=0, tiled=True)  7.56 us
    psum x1, blocking collectives, shards(): summed = lax.psum((running[0], running[1]), ('vir', 'sub'))  6.07 us
    dot_general x8, matrix products, shards(): jnp.einsum('psxz,psyz->sxy', left_block, right_block, preferred_element_t...  5.32 us
    dot_general x4, other arithmetic, share_gram(): lax.dot_general(left_flat, right_flat, (((1,), (1,)), ((), ())), preferre...  3.22 us
  transfers between devices with their start and end apart: 5, of which 3 were waited for; matrix products, arithmetic and copies ran while one was open for 15% of the time, Pallas kernels for 0%

commit v1 on v0

v1 whole, which is shorter than its diff:
```python
import functools
import math

import jax
import jax.numpy as jnp
from jax import lax
from jax.experimental import pallas as pl
from jax.experimental.pallas import tpu as pltpu
from jax.sharding import PartitionSpec as P

OCC = 256
GR = 16
LANES = 128
MESH = pl.DeviceIdType.MESH
F32 = jnp.float32
BF16 = jnp.bfloat16


def tile_table(tile_list, nt, ntv):
    grid = jnp.arange(ntv, dtype=jnp.int32)
    low = jnp.minimum(grid[:, None], grid[None, :])
    high = jnp.maximum(grid[:, None], grid[None, :])
    hit = (tile_list[:, 0][None, None] == low[:, :, None]) & (
        tile_list[:, 1][None, None] == high[:, :, None]
    )
    slots = jnp.arange(nt, dtype=jnp.int32)
    found = jnp.sum(jnp.where(hit, slots[None, None], 0), axis=2)
    return (found + jnp.where(grid[:, None] > grid[None, :], nt, 0)).reshape(-1)


def kernel(dims, amp, pairs, tiles, table, virt, occ, full, tile_buf, ga, acc, msg_s, msg_x,
           msg_z, part, landed, orb_buf, couple_buf,
           x_s, x_r, d_s, d_r, y_s, y_r, a_s, a_r, gs_s, gs_r, gx_s, gx_r, gz_s, gz_r,
           rs_s, rs_r, ag_s, ag_r):
    nz, nx, ns, pd, sd, gs, cg, nt, ntv, nch = dims
    n = nz * pd
    occs = 2 * n
    rd = gs * GR
    tw = ns * rd
    z_at = lax.axis_index("pair")
    x_at = lax.axis_index("vir")
    s_at = lax.axis_index("sub")
    sizes = {"pair": nz, "vir": nx, "sub": ns}
    here = {"pair": z_at, "vir": x_at, "sub": s_at}

    def ahead(axis, by):
        return lax.rem(here[axis] + by, sizes[axis])

    def behind(axis, by):
        return lax.rem(here[axis] + sizes[axis] - by, sizes[axis])

    def send(src, dst, s_sem, r_sem, axis, by):
        return pltpu.make_async_remote_copy(
            src_ref=src, dst_ref=dst, send_sem=s_sem, recv_sem=r_sem,
            device_id={axis: ahead(axis, by)}, device_id_type=MESH)

    barrier = pltpu.get_barrier_semaphore()
    count = 0
    for axis in ("sub", "vir", "pair"):
        for by in range(1, sizes[axis]):
            pl.semaphore_signal(barrier, inc=1, device_id={axis: ahead(axis, by)},
                                device_id_type=MESH)
            count += 1
    pl.semaphore_wait(barrier, count)

    step = sd // nch * gs

    def x_copy(by, ch):
        rows = pl.ds(ch * step, step)
        return send(amp.at[:, rows], full.at[x_at, s_at, :, rows], x_s.at[by - 1, ch],
                    x_r.at[by - 1, ch], "vir", by)

    def relay(by, hop, ch):
        rows = pl.ds(ch * step, step)
        at = full.at[behind("vir", by), s_at, :, rows]
        return send(at, at, y_s.at[hop - 1, by - 1, ch], y_r.at[hop - 1, by - 1, ch], "sub", hop)

    def own_copy(hop):
        return send(amp, full.at[x_at, s_at], d_s.at[hop - 1], d_r.at[hop - 1], "sub", hop)

    def a2a_copy(by):
        rows = pl.ds(ahead("pair", by) * cg, cg)
        return send(amp.at[:, rows], ga.at[z_at], a_s.at[by - 1], a_r.at[by - 1], "pair", by)

    for ch in range(nch):
        for by in range(1, nx):
            x_copy(by, ch).start()
    for hop in range(1, ns):
        own_copy(hop).start()
    for by in range(1, nz):
        a2a_copy(by).start()

    full[x_at, s_at] = amp[...]
    ga[z_at] = amp[:, pl.ds(z_at * cg, cg)]
    lane_of = lax.broadcasted_iota(jnp.int32, (tw, LANES), 1)
    row_of = lax.broadcasted_iota(jnp.int32, (tw, LANES), 0)
    lower = lane_of <= row_of

    def build(x_from, lo, hi):
        def one(local, carry):
            slot = x_from * sd + local
            diagonal = tiles[slot, 0] == tiles[slot, 1]
            dropped = lower & diagonal
            groups = pl.ds(local * gs, gs)
            for k in range(pd):
                whole = jnp.concatenate(
                    [full[x_from, s, k, groups].reshape(rd, LANES) for s in range(ns)], axis=0)
                kept = jnp.where(dropped, 0.0, whole.astype(F32))
                turned = kept.T
                tile_buf[k, slot] = (kept - jnp.where(diagonal, turned, 0.0)).astype(BF16)
                tile_buf[k, nt + slot] = (-turned).astype(BF16)
            return carry

        lax.fori_loop(lo, hi, one, 0)

    for hop in range(1, ns):
        own_copy(hop).wait_recv()
    build(x_at, 0, sd)

    for by in range(1, nz):
        a2a_copy(by).wait_recv()
    acc[...] = jnp.zeros_like(acc)
    g_lane = lax.broadcasted_iota(jnp.int32, (GR, LANES), 1)
    g_row = lax.broadcasted_iota(jnp.int32, (GR, LANES), 0)

    def gram_group(i, carry):
        at = z_at * cg + i
        slot = x_at * sd + jnp.minimum(at // gs, sd - 1)
        diagonal = tiles[slot, 0] == tiles[slot, 1]
        dropped = (g_lane <= g_row + (s_at * rd + lax.rem(at, gs) * GR)) & diagonal
        vals = ga[:, :, i].reshape(n, GR, LANES).astype(F32)
        vals = jnp.where(dropped[None], 0.0, vals)
        for p in range(n):
            acc[p] += vals * vals[p : p + 1]
        return carry

    lax.fori_loop(0, cg, gram_group, 0)
    m_lane = lax.broadcasted_iota(jnp.int32, (n, LANES), 1)
    grid = jnp.zeros((n, LANES), F32)
    for p in range(n):
        col = jnp.sum(jnp.sum(acc[p], axis=1), axis=1, keepdims=True)
        grid = jnp.where((m_lane == p) | (m_lane == p + n), col, grid)
    msg_s[0, 0:n] = grid
    msg_s[0, n:occs] = grid

    def gs_copy(hop):
        return send(msg_s.at[0], msg_s.at[hop], gs_s.at[hop - 1], gs_r.at[hop - 1], "sub", hop)

    def gx_copy(by):
        return send(msg_x.at[0], msg_x.at[by], gx_s.at[by - 1], gx_r.at[by - 1], "vir", by)

    def gz_copy(by):
        return send(msg_z.at[z_at], msg_z.at[z_at], gz_s.at[by - 1], gz_r.at[by - 1], "pair", by)

    for hop in range(1, ns):
        gs_copy(hop).start()

    for by in range(1, nx):
        for ch in range(nch):
            x_copy(by, ch).wait_recv()
            for hop in range(1, ns):
                relay(by, hop, ch).start()
            if ch == 0 and by == 1:
                total = msg_s[0]
                for hop in range(1, ns):
                    gs_copy(hop).wait_recv()
                    total = total + msg_s[hop]
                msg_x[0] = total
                for other in range(1, nx):
                    gx_copy(other).start()
            for hop in range(1, ns):
                relay(by, hop, ch).wait_recv()
            build(behind("vir", by), ch * (sd // nch), (ch + 1) * (sd // nch))

    total = msg_x[0]
    for by in range(1, nx):
        gx_copy(by).wait_recv()
        total = total + msg_x[by]
    msg_z[z_at, 0:occs] = total
    for k in range(pd):
        for e in range(2):
            msg_z[z_at, pl.ds(occs + 2 * k + e, 1)] = jnp.full((1, LANES), pairs[k, e], jnp.int32).astype(F32)
    for by in range(1, nz):
        gz_copy(by).start()

    if part.shape[0] > sd * gs:
        part[pl.ds(sd * gs, part.shape[0] - sd * gs)] = jnp.zeros(
            (part.shape[0] - sd * gs, GR, LANES), F32)

    def virt_slot(local, carry):
        slot = x_at * sd + local
        r = tiles[slot, 0]
        c = tiles[slot, 1]
        rows = pl.ds(pl.multiple_of(s_at * rd, rd), rd)
        total = None
        for k in range(pd):
            left = jnp.concatenate(
                [tile_buf[k, table[r * ntv + j], rows] for j in range(ntv)], axis=1)
            right = jnp.concatenate(
                [tile_buf[k, table[j * ntv + c]] for j in range(ntv)], axis=0)
            term = jnp.dot(left, right, preferred_element_type=F32)
            total = term if total is None else total + term
        part[pl.ds(local * gs, gs)] = (-total).reshape(gs, GR, LANES)
        return carry

    lax.fori_loop(0, sd, virt_slot, 0)

    def rs_copy(by):
        rows = pl.ds(ahead("pair", by) * cg, cg)
        return send(part.at[rows], landed.at[by - 1], rs_s.at[by - 1], rs_r.at[by - 1], "pair", by)

    own = pl.ds(z_at * cg, cg)

    def ag_copy(by):
        return send(virt.at[own], virt.at[own], ag_s.at[by - 1], ag_r.at[by - 1], "pair", by)

    for by in range(1, nz):
        rs_copy(by).start()

    for by in range(1, nz):
        gz_copy(by).wait_recv()
    gram = msg_z[0, 0:occs]
    for z in range(1, nz):
        gram = gram + msg_z[z, 0:occs]
    o_lane = lax.broadcasted_iota(jnp.int32, (1, LANES), 1)
    orb_lane = jnp.full((1, LANES), -1.0, F32)
    par_lane = jnp.full((1, LANES), -1.0, F32)
    orb_buf[...] = jnp.full(orb_buf.shape, -1.0, F32)
    for u in range(occs):
        p, e = u % n, u // n
        base = occs + 2 * (p % pd)
        orb = msg_z[p // pd, base + e : base + e + 1]
        par = msg_z[p // pd, base + 1 - e : base + 2 - e]
        orb_lane = jnp.where(o_lane == u, orb, orb_lane)
        par_lane = jnp.where(o_lane == u, par, par_lane)
        orb_buf[0, u : u + 1] = orb
        orb_buf[1, u : u + 1] = par
    c_lane = lax.broadcasted_iota(jnp.int32, (occs, LANES), 1)
    c_row = lax.broadcasted_iota(jnp.int32, (occs, LANES), 0)
    signed = jnp.where((c_lane < n) == (c_row < n), -gram, gram)
    couple_buf[...] = jnp.zeros_like(couple_buf)
    couple_buf[0:occs] = jnp.where(orb_buf[1, 0:occs] == par_lane, signed, 0.0)
    right_hot = (jnp.concatenate([orb_buf[0]] * (OCC // LANES), axis=1)
                 == lax.broadcasted_iota(jnp.int32, (LANES, OCC), 1).astype(F32)).astype(F32)
    left_hot = (lax.broadcasted_iota(jnp.int32, (OCC, LANES), 0).astype(F32)
                == orb_lane).astype(F32)
    inner = jnp.dot(couple_buf[...], right_hot, precision=lax.Precision.HIGHEST,
                    preferred_element_type=F32)
    occ[...] = jnp.dot(left_hot, inner, precision=lax.Precision.HIGHEST,
                       preferred_element_type=F32)

    for by in range(1, nz):
        rs_copy(by).wait_recv()
    total = part[own]
    for by in range(1, nz):
        total = total + landed[by - 1]
    virt[own] = total
    for by in range(1, nz):
        ag_copy(by).start()
    for by in range(1, nz):
        ag_copy(by).wait_recv()

    for by in range(1, nx):
        gx_copy(by).wait_send()
        for ch in range(nch):
            x_copy(by, ch).wait_send()
            for hop in range(1, ns):
                relay(by, hop, ch).wait_send()
    for hop in range(1, ns):
        own_copy(hop).wait_send()
        gs_copy(hop).wait_send()
    for by in range(1, nz):
        a2a_copy(by).wait_send()
        gz_copy(by).wait_send()
        rs_copy(by).wait_send()
        ag_copy(by).wait_send()


def shards(sizes, amplitudes, pair_list, tile_list):
    nz, nx, ns = sizes
    pd, sd, rd, _ = amplitudes.shape
    nt = tile_list.shape[0]
    ntv = (math.isqrt(8 * nt + 1) - 1) // 2
    gs = rd // GR
    ng = sd * gs
    cg = -(-ng // nz)
    ngp = cg * nz
    nch = 3 if sd % 3 == 0 else 1
    n = nz * pd
    occs = 2 * n
    amp = amplitudes.reshape(pd, ng, GR, LANES)
    if ngp > ng:
        amp = jnp.pad(amp, ((0, 0), (0, ngp - ng), (0, 0), (0, 0)))
    mr = -(-(occs + 2 * pd) // 8) * 8
    dims = (nz, nx, ns, pd, sd, gs, cg, nt, ntv, nch)
    vmem = pl.BlockSpec(memory_space=pltpu.VMEM)
    smem = pl.BlockSpec(memory_space=pltpu.SMEM)

    def dma(*shape):
        return pltpu.SemaphoreType.DMA(tuple(max(1, d) for d in shape))

    sems = []
    for shape in ((nx - 1, nch), (ns - 1,), (ns - 1, nx - 1, nch), (nz - 1,), (ns - 1,),
                  (nx - 1,), (nz - 1,), (nz - 1,), (nz - 1,)):
        sems += [dma(*shape), dma(*shape)]
    virt, occ = pl.pallas_call(
        functools.partial(kernel, dims),
        out_shape=(jax.ShapeDtypeStruct((ngp, GR, LANES), F32),
                   jax.ShapeDtypeStruct((OCC, OCC), F32)),
        in_specs=[vmem, smem, smem, smem],
        out_specs=(vmem, vmem),
        scratch_shapes=[
            pltpu.VMEM((nx, ns, pd, ngp, GR, LANES), BF16),
            pltpu.VMEM((pd, 2 * nt, ns * rd, LANES), BF16),
            pltpu.VMEM((nz, pd, cg, GR, LANES), BF16),
            pltpu.VMEM((n, n, GR, LANES), F32),
            pltpu.VMEM((ns, occs, LANES), F32),
            pltpu.VMEM((nx, occs, LANES), F32),
            pltpu.VMEM((nz, mr, LANES), F32),
            pltpu.VMEM((ngp, GR, LANES), F32),
            pltpu.VMEM((max(1, nz - 1), cg, GR, LANES), F32),
            pltpu.VMEM((2, LANES, LANES), F32),
            pltpu.VMEM((LANES, LANES), F32),
            *sems,
        ],
        compiler_params=pltpu.CompilerParams(
            collective_id=0, has_side_effects=True, vmem_limit_bytes=48 * 1024 * 1024),
    )(amp, pair_list, tile_list, tile_table(tile_list, nt, ntv))
    return (virt[:ng].reshape(sd, rd, LANES), occ)


def solution(mesh):
    in_specs = (P(("groups", "pair"), "vir", "sub", None), P(("groups", "pair"), None), P())
    out_specs = (P(("groups", "vir"), "sub", None), P("groups", None))
    sizes = (mesh.shape["pair"], mesh.shape["vir"], mesh.shape["sub"])
    return jax.shard_map(functools.partial(shards, sizes), mesh=mesh, in_specs=in_specs,
                         out_specs=out_specs, check_vma=False)
```

time: 148 us -> 52.7 us (0.36)
  the two profiles are of different devices: /device:TPU:0 before, /device:TPU:25 now
where the time goes in v1:
time: 52.7 us; the launch traced here: 52.5 us
  Pallas kernels  47.6 us (90%)
  local copies, waits for them, and re-layouts  3.9 us (7%)
  between operations  0.66 us (1%)
    pallas_call x1, Pallas kernels, shards(): pl.pallas_call(functools.partial(kernel, dims), out_shape=(jax.ShapeDtype...  47.6 us
    unnamed x9, local copies, waits for them, and re-layouts  3.82 us

profile of v1, /device:TPU:25, one launch (start us, length us, event | category | flops | bytes accessed | tf_op | source)
XLA Modules:
  0.0 52.5 jit_solution(9622851928805941904)
XLA Ops:
  0.6 0.0 copy-start.2
  0.6 0.7 %copy-done.2 = s32[36,2]{0,1:T(2,128)S(1)} copy-done((s32[36,2]{0,1:T(2,128)S(1)}, s32[36,2]{0,1:T(2,128)}, u32[]{:S(2)}) %copy-start.2) | copy-done | bytes 312
  1.3 0.3 select_reduce_fusion
  1.6 0.1 add.8.table
  1.7 0.0 copy-start.1
  1.7 0.1 copy.6.tiles
  1.8 0.6 %copy-done.1 = s32[1,2]{1,0:T(1,128)S(1)} copy-done((s32[1,2]{1,0:T(1,128)S(1)}, s32[1,2]{1,0:T(1,128)}, u32[]{:S(2)}) %copy-start.1) | copy-done | bytes 32
  2.4 0.0 copy-start
  2.4 1.0 %copy-done = bf16[1,18,64,128]{3,2,1,0:T(8,128)(2,1)S(1)} copy-done((bf16[1,18,64,128]{3,2,1,0:T(8,128)(2,1)S(1)}, bf16[1,18,64,128]{3,2,1,0:T(8,128)(2,1)}, u32[]{:S(2)}) %copy-start) | copy-done | bytes 294936
  3.3 47.6 %shard_map.50 = (f32[72,16,128]{2,1,0:T(8,128)S(1)}, f32[256,256]{1,0:T(8,128)S(1)}) custom-call(bf16[1,72,16,128]{3,2,1,0:T(8,128)(2,1)S(1)} %bitcast.7, s32[1,2]{1,0:T(1,128)S(1)} %copy-done.1, s32[36,2]{1,0:T(8,128)S(1)} %copy.6.tiles, s32[64]{0:T(128)S(1)} %add.8.table), custom_call_target="tpu_custom_call" | custom-call | tf_op jit(solution)/shard_map/pallas_call | solution.py:306
  51.0 0.8 %copy.9 = f32[18,64,128]{2,1,0:T(8,128)} copy(f32[18,64,128]{2,1,0:T(8,128)S(1)} %bitcast.6) | data formatting | bytes 1179648
  51.8 0.7 %copy.10 = f32[256,256]{1,0:T(8,128)} copy(f32[256,256]{1,0:T(8,128)S(1)} %get-tuple-element.13) | data formatting | bytes 524288
  (3 shorter events, 0.0 us)
Async XLA Ops:
  0.6 0.7 %copy-start.2 = (s32[36,2]{0,1:T(2,128)S(1)}, s32[36,2]{0,1:T(2,128)}, u32[]{:S(2)}) copy-start(s32[36,2]{0,1:T(2,128)} %param.5) | copy-start | bytes 868
  1.7 0.7 %copy-start.1 = (s32[1,2]{1,0:T(1,128)S(1)}, s32[1,2]{1,0:T(1,128)}, u32[]{:S(2)}) copy-start(s32[1,2]{1,0:T(1,128)} %pairs.1) | copy-start | bytes 28
  2.4 1.0 %copy-start = (bf16[1,18,64,128]{3,2,1,0:T(8,128)(2,1)S(1)}, bf16[1,18,64,128]{3,2,1,0:T(8,128)(2,1)}, u32[]{:S(2)}) copy-start(bf16[1,18,64,128]{3,2,1,0:T(8,128)(2,1)} %param.3) | copy-start | bytes 884740

commit v2 on v1

--- a/solution.py
+++ b/solution.py
@@ -11,6 +11,7 @@
 OCC = 256
 GR = 16
 LANES = 128
+LEVELS = 32767.0
 MESH = pl.DeviceIdType.MESH
 F32 = jnp.float32
 BF16 = jnp.bfloat16
@@ -28,10 +29,20 @@
     return (found + jnp.where(grid[:, None] > grid[None, :], nt, 0)).reshape(-1)
 
 
-def kernel(dims, amp, pairs, tiles, table, virt, occ, full, tile_buf, ga, acc, msg_s, msg_x,
-           msg_z, part, landed, orb_buf, couple_buf,
-           x_s, x_r, d_s, d_r, y_s, y_r, a_s, a_r, gs_s, gs_r, gx_s, gx_r, gz_s, gz_r,
-           rs_s, rs_r, ag_s, ag_r):
+def squeeze(vals):
+    peak = jnp.maximum(jnp.max(jnp.abs(vals), axis=1, keepdims=True), 1e-33)
+    whole = jnp.round(vals * (LEVELS / peak)).astype(jnp.int32)
+    return whole.astype(jnp.int16), peak * (1.0 / LEVELS)
+
+
+def widen(whole, scale):
+    return whole.astype(jnp.int32).astype(F32) * scale
+
+
+def kernel(dims, amp_in, pairs, tiles, table, fin, fin_scale, occ, amp, full, tile_buf, ga, acc,
+           msg_s, msg_x, msg_z, part, part_q, part_scale, landed, landed_scale, orb_buf,
+           couple_buf, in_sem, x_s, x_r, d_s, d_r, y_s, y_r, a_s, a_r, gs_s, gs_r, gx_s, gx_r, gz_s, gz_r,
+           rs_s, rs_r, ag_s, ag_r, rt_s, rt_r, at_s, at_r):
     nz, nx, ns, pd, sd, gs, cg, nt, ntv, nch = dims
     n = nz * pd
     occs = 2 * n
@@ -54,6 +65,8 @@
             src_ref=src, dst_ref=dst, send_sem=s_sem, recv_sem=r_sem,
             device_id={axis: ahead(axis, by)}, device_id_type=MESH)
 
+    fetch = pltpu.make_async_copy(amp_in, amp, in_sem)
+    fetch.start()
     barrier = pltpu.get_barrier_semaphore()
     count = 0
     for axis in ("sub", "vir", "pair"):
@@ -62,6 +75,7 @@
                                 device_id_type=MESH)
             count += 1
     pl.semaphore_wait(barrier, count)
+    fetch.wait()
 
     step = sd // nch * gs
 
@@ -117,75 +131,20 @@
         own_copy(hop).wait_recv()
     build(x_at, 0, sd)
 
-    for by in range(1, nz):
-        a2a_copy(by).wait_recv()
-    acc[...] = jnp.zeros_like(acc)
-    g_lane = lax.broadcasted_iota(jnp.int32, (GR, LANES), 1)
-    g_row = lax.broadcasted_iota(jnp.int32, (GR, LANES), 0)
-
-    def gram_group(i, carry):
-        at = z_at * cg + i
-        slot = x_at * sd + jnp.minimum(at // gs, sd - 1)
-        diagonal = tiles[slot, 0] == tiles[slot, 1]
-        dropped = (g_lane <= g_row + (s_at * rd + lax.rem(at, gs) * GR)) & diagonal
-        vals = ga[:, :, i].reshape(n, GR, LANES).astype(F32)
-        vals = jnp.where(dropped[None], 0.0, vals)
-        for p in range(n):
-            acc[p] += vals * vals[p : p + 1]
-        return carry
-
-    lax.fori_loop(0, cg, gram_group, 0)
-    m_lane = lax.broadcasted_iota(jnp.int32, (n, LANES), 1)
-    grid = jnp.zeros((n, LANES), F32)
-    for p in range(n):
-        col = jnp.sum(jnp.sum(acc[p], axis=1), axis=1, keepdims=True)
-        grid = jnp.where((m_lane == p) | (m_lane == p + n), col, grid)
-    msg_s[0, 0:n] = grid
-    msg_s[0, n:occs] = grid
-
-    def gs_copy(hop):
-        return send(msg_s.at[0], msg_s.at[hop], gs_s.at[hop - 1], gs_r.at[hop - 1], "sub", hop)
-
-    def gx_copy(by):
-        return send(msg_x.at[0], msg_x.at[by], gx_s.at[by - 1], gx_r.at[by - 1], "vir", by)
-
-    def gz_copy(by):
-        return send(msg_z.at[z_at], msg_z.at[z_at], gz_s.at[by - 1], gz_r.at[by - 1], "pair", by)
-
-    for hop in range(1, ns):
-        gs_copy(hop).start()
-
     for by in range(1, nx):
         for ch in range(nch):
             x_copy(by, ch).wait_recv()
             for hop in range(1, ns):
                 relay(by, hop, ch).start()
-            if ch == 0 and by == 1:
-                total = msg_s[0]
-                for hop in range(1, ns):
-                    gs_copy(hop).wait_recv()
-                    total = total + msg_s[hop]
-                msg_x[0] = total
-                for other in range(1, nx):
-                    gx_copy(other).start()
             for hop in range(1, ns):
                 relay(by, hop, ch).wait_recv()
             build(behind("vir", by), ch * (sd // nch), (ch + 1) * (sd // nch))
 
-    total = msg_x[0]
-    for by in range(1, nx):
-        gx_copy(by).wait_recv()
-        total = total + msg_x[by]
-    msg_z[z_at, 0:occs] = total
-    for k in range(pd):
-        for e in range(2):
-            msg_z[z_at, pl.ds(occs + 2 * k + e, 1)] = jnp.full((1, LANES), pairs[k, e], jnp.int32).astype(F32)
-    for by in range(1, nz):
-        gz_copy(by).start()
-
     if part.shape[0] > sd * gs:
-        part[pl.ds(sd * gs, part.shape[0] - sd * gs)] = jnp.zeros(
-            (part.shape[0] - sd * gs, GR, LANES), F32)
+        spare = pl.ds(sd * gs, part.shape[0] - sd * gs)
+        part[spare] = jnp.zeros((part.shape[0] - sd * gs, GR, LANES), F32)
+        part_q[spare] = jnp.zeros((part.shape[0] - sd * gs, GR, LANES), jnp.int16)
+        part_scale[spare] = jnp.zeros((part.shape[0] - sd * gs, 1, LANES), F32)
 
     def virt_slot(local, carry):
         slot = x_at * sd + local
@@ -200,22 +159,106 @@
                 [tile_buf[k, table[j * ntv + c]] for j in range(ntv)], axis=0)
             term = jnp.dot(left, right, preferred_element_type=F32)
             total = term if total is None else total + term
-        part[pl.ds(local * gs, gs)] = (-total).reshape(gs, GR, LANES)
+        groups = pl.ds(local * gs, gs)
+        total = (-total).reshape(gs, GR, LANES)
+        part[groups] = total
+        part_q[groups], part_scale[groups] = squeeze(total)
         return carry
 
-    lax.fori_loop(0, sd, virt_slot, 0)
-
-    def rs_copy(by):
-        rows = pl.ds(ahead("pair", by) * cg, cg)
-        return send(part.at[rows], landed.at[by - 1], rs_s.at[by - 1], rs_r.at[by - 1], "pair", by)
+    def rs_copies(to, source):
+        rows = pl.ds(to * cg, cg)
+        return [
+            pltpu.make_async_remote_copy(
+                src_ref=src.at[rows], dst_ref=dst.at[source], send_sem=s_sem.at[to],
+                recv_sem=r_sem.at[source], device_id={"pair": to}, device_id_type=MESH)
+            for src, dst, s_sem, r_sem in ((part_q, landed, rs_s, rs_r),
+                                           (part_scale, landed_scale, rt_s, rt_r))
+        ]
 
     own = pl.ds(z_at * cg, cg)
 
-    def ag_copy(by):
-        return send(virt.at[own], virt.at[own], ag_s.at[by - 1], ag_r.at[by - 1], "pair", by)
-
-    for by in range(1, nz):
-        rs_copy(by).start()
+    def ag_copies(by):
+        return [
+            send(ref.at[own], ref.at[own], s_sem.at[by - 1], r_sem.at[by - 1], "pair", by)
+            for ref, s_sem, r_sem in ((fin, ag_s, ag_r), (fin_scale, at_s, at_r))
+        ]
+
+    done = 0
+    for to in range(nz):
+        until = min(sd, -(-cg * (to + 1) // gs))
+        if until > done:
+            lax.fori_loop(done, until, virt_slot, 0)
+            done = until
+
+        @pl.when(z_at != to)
+        def _():
+            for copy in rs_copies(to, z_at):
+                copy.start()
+
+    for by in range(1, nz):
+        a2a_copy(by).wait_recv()
+    acc[...] = jnp.zeros_like(acc)
+    g_lane = lax.broadcasted_iota(jnp.int32, (GR, LANES), 1)
+    g_row = lax.broadcasted_iota(jnp.int32, (GR, LANES), 0)
+
+    def gram_group(i, carry):
+        at = z_at * cg + i
+        slot = x_at * sd + jnp.minimum(at // gs, sd - 1)
+        diagonal = tiles[slot, 0] == tiles[slot, 1]
+        dropped = (g_lane <= g_row + (s_at * rd + lax.rem(at, gs) * GR)) & diagonal
+        vals = ga[:, :, i].reshape(n, GR, LANES).astype(F32)
+        vals = jnp.where(dropped[None], 0.0, vals)
+        for p in range(n):
+            acc[p] += vals * vals[p : p + 1]
+        return carry
+
+    lax.fori_loop(0, cg, gram_group, 0)
+    m_lane = lax.broadcasted_iota(jnp.int32, (n, LANES), 1)
+    grid = jnp.zeros((n, LANES), F32)
+    for p in range(n):
+        col = jnp.sum(jnp.sum(acc[p], axis=1), axis=1, keepdims=True)
+        grid = jnp.where((m_lane == p) | (m_lane == p + n), col, grid)
+    msg_s[0, 0:n] = grid
+    msg_s[0, n:occs] = grid
+
+    def gs_copy(hop):
+        return send(msg_s.at[0], msg_s.at[hop], gs_s.at[hop - 1], gs_r.at[hop - 1], "sub", hop)
+
+    def gx_copy(by):
+        return send(msg_x.at[0], msg_x.at[by], gx_s.at[by - 1], gx_r.at[by - 1], "vir", by)
+
+    def gz_copy(by):
+        return send(msg_z.at[z_at], msg_z.at[z_at], gz_s.at[by - 1], gz_r.at[by - 1], "pair", by)
+
+    for hop in range(1, ns):
+        gs_copy(hop).start()
+
+    for hop in range(1, ns):
+        gs_copy(hop).wait_recv()
+    msg_x[0] = sum((msg_s[hop] for hop in range(1, ns)), msg_s[0])
+    for by in range(1, nx):
+        gx_copy(by).start()
+    total = msg_x[0]
+    for by in range(1, nx):
+        gx_copy(by).wait_recv()
+        total = total + msg_x[by]
+    msg_z[z_at, 0:occs] = total
+    for k in range(pd):
+        for e in range(2):
+            msg_z[z_at, pl.ds(occs + 2 * k + e, 1)] = jnp.full((1, LANES), pairs[k, e], jnp.int32).astype(F32)
+    for by in range(1, nz):
+        gz_copy(by).start()
+
+    total = part[own]
+    for by in range(1, nz):
+        source = behind("pair", by)
+        for copy in rs_copies(source, source):
+            copy.wait_recv()
+        total = total + widen(landed[source], landed_scale[source])
+    fin[own], fin_scale[own] = squeeze(total)
+    for by in range(1, nz):
+        for copy in ag_copies(by):
+            copy.start()
 
     for by in range(1, nz):
         gz_copy(by).wait_recv()
@@ -250,15 +293,8 @@
                        preferred_element_type=F32)
 
     for by in range(1, nz):
-        rs_copy(by).wait_recv()
-    total = part[own]
-    for by in range(1, nz):
-        total = total + landed[by - 1]
-    virt[own] = total
-    for by in range(1, nz):
-        ag_copy(by).start()
-    for by in range(1, nz):
-        ag_copy(by).wait_recv()
+        for copy in ag_copies(by):
+            copy.wait_recv()
 
     for by in range(1, nx):
         gx_copy(by).wait_send()
@@ -272,8 +308,8 @@
     for by in range(1, nz):
         a2a_copy(by).wait_send()
         gz_copy(by).wait_send()
-        rs_copy(by).wait_send()
-        ag_copy(by).wait_send()
+        for copy in ag_copies(by) + rs_copies(ahead("pair", by), z_at):
+            copy.wait_send()
 
 
 def shards(sizes, amplitudes, pair_list, tile_list):
@@ -285,7 +321,7 @@
     ng = sd * gs
     cg = -(-ng // nz)
     ngp = cg * nz
-    nch = 3 if sd % 3 == 0 else 1
+    nch = 6 if sd % 6 == 0 else 3 if sd % 3 == 0 else 1
     n = nz * pd
     occs = 2 * n
     amp = amplitudes.reshape(pd, ng, GR, LANES)
@@ -301,15 +337,17 @@
 
     sems = []
     for shape in ((nx - 1, nch), (ns - 1,), (ns - 1, nx - 1, nch), (nz - 1,), (ns - 1,),
-                  (nx - 1,), (nz - 1,), (nz - 1,), (nz - 1,)):
+                  (nx - 1,), (nz - 1,), (nz,), (nz - 1,), (nz,), (nz - 1,)):
         sems += [dma(*shape), dma(*shape)]
-    virt, occ = pl.pallas_call(
+    fin, scale, occ = pl.pallas_call(
         functools.partial(kernel, dims),
-        out_shape=(jax.ShapeDtypeStruct((ngp, GR, LANES), F32),
+        out_shape=(jax.ShapeDtypeStruct((ngp, GR, LANES), jnp.int16),
+                   jax.ShapeDtypeStruct((ngp, 1, LANES), F32),
                    jax.ShapeDtypeStruct((OCC, OCC), F32)),
-        in_specs=[vmem, smem, smem, smem],
-        out_specs=(vmem, vmem),
+        in_specs=[pl.BlockSpec(memory_space=pl.ANY), smem, smem, smem],
+        out_specs=(vmem, vmem, vmem),
         scratch_shapes=[
+            pltpu.VMEM((pd, ngp, GR, LANES), BF16),
             pltpu.VMEM((nx, ns, pd, ngp, GR, LANES), BF16),
             pltpu.VMEM((pd, 2 * nt, ns * rd, LANES), BF16),
             pltpu.VMEM((nz, pd, cg, GR, LANES), BF16),
@@ -318,15 +356,20 @@
             pltpu.VMEM((nx, occs, LANES), F32),
             pltpu.VMEM((nz, mr, LANES), F32),
             pltpu.VMEM((ngp, GR, LANES), F32),
-            pltpu.VMEM((max(1, nz - 1), cg, GR, LANES), F32),
+            pltpu.VMEM((ngp, GR, LANES), jnp.int16),
+            pltpu.VMEM((ngp, 1, LANES), F32),
+            pltpu.VMEM((nz, cg, GR, LANES), jnp.int16),
+            pltpu.VMEM((nz, cg, 1, LANES), F32),
             pltpu.VMEM((2, LANES, LANES), F32),
             pltpu.VMEM((LANES, LANES), F32),
+            pltpu.SemaphoreType.DMA,
             *sems,
         ],
         compiler_params=pltpu.CompilerParams(
             collective_id=0, has_side_effects=True, vmem_limit_bytes=48 * 1024 * 1024),
     )(amp, pair_list, tile_list, tile_table(tile_list, nt, ntv))
-    return (virt[:ng].reshape(sd, rd, LANES), occ)
+    virt = fin[:ng].astype(F32) * scale[:ng]
+    return (virt.reshape(sd, rd, LANES), occ)
 
 
 def solution(mesh):

time: 52.7 us -> 44.6 us (0.85)
  the two profiles are of different devices: /device:TPU:25 before, /device:TPU:0 now
where the time goes in v2:
time: 44.6 us; the launch traced here: 44.4 us
  Pallas kernels  39.5 us (89%)
  local copies, waits for them, and re-layouts  3.08 us (7%)
  other arithmetic  1.2 us (3%)
  between operations  0.66 us (1%)
    pallas_call x1, Pallas kernels, shards(): pl.pallas_call(functools.partial(kernel, dims), out_shape=(jax.ShapeDtype...  39.5 us
    unnamed x8, local copies, waits for them, and re-layouts  3 us
    mul x1, other arithmetic, shards(): virt = fin[:ng].astype(F32) * scale[:ng]  0.91 us

profile of v2, /device:TPU:0, one launch (start us, length us, event | category | flops | bytes accessed | tf_op | source)
XLA Modules:
  0.0 44.4 jit_solution(8922790169020786392)
XLA Ops:
  0.6 0.0 copy-start.2
  0.6 0.7 %copy-done.2 = s32[36,2]{0,1:T(2,128)S(1)} copy-done((s32[36,2]{0,1:T(2,128)S(1)}, s32[36,2]{0,1:T(2,128)}, u32[]{:S(2)}) %copy-start.2) | copy-done | bytes 312
  1.3 0.3 select_reduce_fusion
  1.6 0.1 add.8.table
  1.7 0.0 copy-start.1
  1.7 0.1 copy.6.tiles
  1.8 0.6 %copy-done.1 = s32[1,2]{1,0:T(1,128)S(1)} copy-done((s32[1,2]{1,0:T(1,128)S(1)}, s32[1,2]{1,0:T(1,128)}, u32[]{:S(2)}) %copy-start.1) | copy-done | bytes 32
  2.4 0.0 copy-start
  2.4 1.0 %copy-done = bf16[1,18,64,128]{3,2,1,0:T(8,128)(2,1)S(1)} copy-done((bf16[1,18,64,128]{3,2,1,0:T(8,128)(2,1)S(1)}, bf16[1,18,64,128]{3,2,1,0:T(8,128)(2,1)}, u32[]{:S(2)}) %copy-start) | copy-done | bytes 294936
  3.3 39.5 %shard_map.50 = (s16[72,16,128]{2,1,0:T(8,128)(2,1)S(1)}, f32[72,1,128]{2,1,0:T(1,128)S(1)}, f32[256,256]{1,0:T(8,128)S(1)}) custom-call(bf16[1,72,16,128]{3,2,1,0:T(8,128)(2,1)S(1)} %bitcast.7, s32[1,2]{1,0:T(1,128)S(1)} %copy-done.1, s32[36,2]{1,0:T(8,128)S(1)} %copy.6.tiles, s32[64]{0:T(128)S(1)} %add.8.table), custom_call_target="tpu_custom_call" | custom-call | tf_op jit(solution)/shard_map/pallas_call | solution.py:342
  42.8 0.9 %convert_multiply_fusion = f32[72,16,128]{2,1,0:T(8,128)} fusion(s16[72,16,128]{2,1,0:T(8,128)(2,1)S(1)} %get-tuple-element.5, f32[72,128]{1,0:T(8,128)S(1)} %bitcast.8), kind=kLoop, calls=%fused_computation | loop fusion | flops 294912 | bytes 921600 | tf_op jit(solution)/shard_map/mul | solution.py:371
  43.7 0.7 %copy.8 = f32[256,256]{1,0:T(8,128)} copy(f32[256,256]{1,0:T(8,128)S(1)} %get-tuple-element.15) | data formatting | bytes 524288
  (3 shorter events, 0.0 us)
Async XLA Ops:
  0.6 0.7 %copy-start.2 = (s32[36,2]{0,1:T(2,128)S(1)}, s32[36,2]{0,1:T(2,128)}, u32[]{:S(2)}) copy-start(s32[36,2]{0,1:T(2,128)} %param.5) | copy-start | bytes 868
  1.7 0.7 %copy-start.1 = (s32[1,2]{1,0:T(1,128)S(1)}, s32[1,2]{1,0:T(1,128)}, u32[]{:S(2)}) copy-start(s32[1,2]{1,0:T(1,128)} %pairs.1) | copy-start | bytes 28
  2.4 1.0 %copy-start = (bf16[1,18,64,128]{3,2,1,0:T(8,128)(2,1)S(1)}, bf16[1,18,64,128]{3,2,1,0:T(8,128)(2,1)}, u32[]{:S(2)}) copy-start(bf16[1,18,64,128]{3,2,1,0:T(8,128)(2,1)} %param.3) | copy-start | bytes 884740

commit v3 on v2

--- a/solution.py
+++ b/solution.py
@@ -43,7 +43,7 @@
            msg_s, msg_x, msg_z, part, part_q, part_scale, landed, landed_scale, orb_buf,
            couple_buf, in_sem, x_s, x_r, d_s, d_r, y_s, y_r, a_s, a_r, gs_s, gs_r, gx_s, gx_r, gz_s, gz_r,
            rs_s, rs_r, ag_s, ag_r, rt_s, rt_r, at_s, at_r):
-    nz, nx, ns, pd, sd, gs, cg, nt, ntv, nch = dims
+    nz, nx, ns, pd, sd, gs, cg, nt, ntv, nch, waves = dims
     n = nz * pd
     occs = 2 * n
     rd = gs * GR
@@ -165,21 +165,23 @@
         part_q[groups], part_scale[groups] = squeeze(total)
         return carry
 
-    def rs_copies(to, source):
-        rows = pl.ds(to * cg, cg)
+    half = cg // waves
+
+    def rs_copies(to, source, wave):
+        rows = pl.ds(to * cg + wave * half, half)
         return [
             pltpu.make_async_remote_copy(
-                src_ref=src.at[rows], dst_ref=dst.at[source], send_sem=s_sem.at[to],
-                recv_sem=r_sem.at[source], device_id={"pair": to}, device_id_type=MESH)
+                src_ref=src.at[rows], dst_ref=dst.at[source, pl.ds(wave * half, half)],
+                send_sem=s_sem.at[to, wave], recv_sem=r_sem.at[source, wave], device_id={"pair": to}, device_id_type=MESH)
             for src, dst, s_sem, r_sem in ((part_q, landed, rs_s, rs_r),
                                            (part_scale, landed_scale, rt_s, rt_r))
         ]
 
-    own = pl.ds(z_at * cg, cg)
-
-    def ag_copies(by):
+    def ag_copies(by, wave):
+        own = pl.ds(z_at * cg + wave * half, half)
         return [
-            send(ref.at[own], ref.at[own], s_sem.at[by - 1], r_sem.at[by - 1], "pair", by)
+            send(ref.at[own], ref.at[own], s_sem.at[by - 1, wave], r_sem.at[by - 1, wave],
+                 "pair", by)
             for ref, s_sem, r_sem in ((fin, ag_s, ag_r), (fin_scale, at_s, at_r))
         ]
 
@@ -192,7 +194,12 @@
 
         @pl.when(z_at != to)
         def _():
-            for copy in rs_copies(to, z_at):
+            for copy in rs_copies(to, z_at, 0):
+                copy.start()
+
+    for wave in range(1, waves):
+        for by in range(1, nz):
+            for copy in rs_copies(ahead("pair", by), z_at, wave):
                 copy.start()
 
     for by in range(1, nz):
@@ -249,16 +256,19 @@
     for by in range(1, nz):
         gz_copy(by).start()
 
-    total = part[own]
-    for by in range(1, nz):
-        source = behind("pair", by)
-        for copy in rs_copies(source, source):
-            copy.wait_recv()
-        total = total + widen(landed[source], landed_scale[source])
-    fin[own], fin_scale[own] = squeeze(total)
-    for by in range(1, nz):
-        for copy in ag_copies(by):
-            copy.start()
+    for wave in range(waves):
+        own = pl.ds(z_at * cg + wave * half, half)
+        total = part[own]
+        for by in range(1, nz):
+            source = behind("pair", by)
+            for copy in rs_copies(source, source, wave):
+                copy.wait_recv()
+            rows = pl.ds(wave * half, half)
+            total = total + widen(landed[source, rows], landed_scale[source, rows])
+        fin[own], fin_scale[own] = squeeze(total)
+        for by in range(1, nz):
+            for copy in ag_copies(by, wave):
+                copy.start()
 
     for by in range(1, nz):
         gz_copy(by).wait_recv()
@@ -293,8 +303,9 @@
                        preferred_element_type=F32)
 
     for by in range(1, nz):
-        for copy in ag_copies(by):
-            copy.wait_recv()
+        for wave in range(waves):
+            for copy in ag_copies(by, wave):
+                copy.wait_recv()
 
     for by in range(1, nx):
         gx_copy(by).wait_send()
@@ -308,8 +319,9 @@
     for by in range(1, nz):
         a2a_copy(by).wait_send()
         gz_copy(by).wait_send()
-        for copy in ag_copies(by) + rs_copies(ahead("pair", by), z_at):
-            copy.wait_send()
+        for wave in range(waves):
+            for copy in ag_copies(by, wave) + rs_copies(ahead("pair", by), z_at, wave):
+                copy.wait_send()
 
 
 def shards(sizes, amplitudes, pair_list, tile_list):
@@ -328,7 +340,8 @@
     if ngp > ng:
         amp = jnp.pad(amp, ((0, 0), (0, ngp - ng), (0, 0), (0, 0)))
     mr = -(-(occs + 2 * pd) // 8) * 8
-    dims = (nz, nx, ns, pd, sd, gs, cg, nt, ntv, nch)
+    waves = 2 if cg % 2 == 0 else 1
+    dims = (nz, nx, ns, pd, sd, gs, cg, nt, ntv, nch, waves)
     vmem = pl.BlockSpec(memory_space=pltpu.VMEM)
     smem = pl.BlockSpec(memory_space=pltpu.SMEM)
 
@@ -337,14 +350,15 @@
 
     sems = []
     for shape in ((nx - 1, nch), (ns - 1,), (ns - 1, nx - 1, nch), (nz - 1,), (ns - 1,),
-                  (nx - 1,), (nz - 1,), (nz,), (nz - 1,), (nz,), (nz - 1,)):
+                  (nx - 1,), (nz - 1,), (nz, waves), (nz - 1, waves), (nz, waves),
+                  (nz - 1, waves)):
         sems += [dma(*shape), dma(*shape)]
     fin, scale, occ = pl.pallas_call(
         functools.partial(kernel, dims),
         out_shape=(jax.ShapeDtypeStruct((ngp, GR, LANES), jnp.int16),
                    jax.ShapeDtypeStruct((ngp, 1, LANES), F32),
                    jax.ShapeDtypeStruct((OCC, OCC), F32)),
-        in_specs=[pl.BlockSpec(memory_space=pl.ANY), smem, smem, smem],
+        in_specs=[pl.BlockSpec(memory_space=pltpu.MemorySpace.HBM), smem, smem, smem],
         out_specs=(vmem, vmem, vmem),
         scratch_shapes=[
             pltpu.VMEM((pd, ngp, GR, LANES), BF16),

time: 44.6 us -> 44.3 us (level)
  no operation moved by 1% of the time
where the time goes in v3:
time: 44.3 us; the launch traced here: 44.1 us
  Pallas kernels  39.1 us (88%)
  local copies, waits for them, and re-layouts  3.08 us (7%)
  other arithmetic  1.2 us (3%)
  between operations  0.66 us (1%)
    pallas_call x1, Pallas kernels, shards(): pl.pallas_call(functools.partial(kernel, dims), out_shape=(jax.ShapeDtype...  39.1 us
    unnamed x8, local copies, waits for them, and re-layouts  3 us
    mul x1, other arithmetic, shards(): virt = fin[:ng].astype(F32) * scale[:ng]  0.91 us

profile of v3, /device:TPU:0, one launch (start us, length us, event | category | flops | bytes accessed | tf_op | source)
XLA Modules:
  0.0 44.1 jit_solution(15893707057508000517)
XLA Ops:
  0.6 0.0 copy-start.2
  0.6 0.7 %copy-done.2 = s32[36,2]{0,1:T(2,128)S(1)} copy-done((s32[36,2]{0,1:T(2,128)S(1)}, s32[36,2]{0,1:T(2,128)}, u32[]{:S(2)}) %copy-start.2) | copy-done | bytes 312
  1.3 0.3 select_reduce_fusion
  1.6 0.1 add.8.table
  1.7 0.0 copy-start.1
  1.7 0.1 copy.6.tiles
  1.8 0.6 %copy-done.1 = s32[1,2]{1,0:T(1,128)S(1)} copy-done((s32[1,2]{1,0:T(1,128)S(1)}, s32[1,2]{1,0:T(1,128)}, u32[]{:S(2)}) %copy-start.1) | copy-done | bytes 32
  2.4 0.0 copy-start
  2.4 1.0 %copy-done = bf16[1,18,64,128]{3,2,1,0:T(8,128)(2,1)S(1)} copy-done((bf16[1,18,64,128]{3,2,1,0:T(8,128)(2,1)S(1)}, bf16[1,18,64,128]{3,2,1,0:T(8,128)(2,1)}, u32[]{:S(2)}) %copy-start) | copy-done | bytes 294936
  3.3 39.1 %shard_map.50 = (s16[72,16,128]{2,1,0:T(8,128)(2,1)S(1)}, f32[72,1,128]{2,1,0:T(1,128)S(1)}, f32[256,256]{1,0:T(8,128)S(1)}) custom-call(bf16[1,72,16,128]{3,2,1,0:T(8,128)(2,1)S(1)} %bitcast.7, s32[1,2]{1,0:T(1,128)S(1)} %copy-done.1, s32[36,2]{1,0:T(8,128)S(1)} %copy.6.tiles, s32[64]{0:T(128)S(1)} %add.8.table), custom_call_target="tpu_custom_call" | custom-call | tf_op jit(solution)/shard_map/pallas_call | solution.py:356
  42.5 0.9 %convert_multiply_fusion = f32[72,16,128]{2,1,0:T(8,128)} fusion(s16[72,16,128]{2,1,0:T(8,128)(2,1)S(1)} %get-tuple-element.5, f32[72,128]{1,0:T(8,128)S(1)} %bitcast.8), kind=kLoop, calls=%fused_computation | loop fusion | flops 294912 | bytes 921600 | tf_op jit(solution)/shard_map/mul | solution.py:385
  43.4 0.7 %copy.8 = f32[256,256]{1,0:T(8,128)} copy(f32[256,256]{1,0:T(8,128)S(1)} %get-tuple-element.15) | data formatting | bytes 524288
  (3 shorter events, 0.0 us)
Async XLA Ops:
  0.6 0.7 %copy-start.2 = (s32[36,2]{0,1:T(2,128)S(1)}, s32[36,2]{0,1:T(2,128)}, u32[]{:S(2)}) copy-start(s32[36,2]{0,1:T(2,128)} %param.5) | copy-start | bytes 868
  1.7 0.7 %copy-start.1 = (s32[1,2]{1,0:T(1,128)S(1)}, s32[1,2]{1,0:T(1,128)}, u32[]{:S(2)}) copy-start(s32[1,2]{1,0:T(1,128)} %pairs.1) | copy-start | bytes 28
  2.4 1.0 %copy-start = (bf16[1,18,64,128]{3,2,1,0:T(8,128)(2,1)S(1)}, bf16[1,18,64,128]{3,2,1,0:T(8,128)(2,1)}, u32[]{:S(2)}) copy-start(bf16[1,18,64,128]{3,2,1,0:T(8,128)(2,1)} %param.3) | copy-start | bytes 884740

commit v4 on v3

--- a/solution.py
+++ b/solution.py
@@ -245,17 +245,6 @@
     msg_x[0] = sum((msg_s[hop] for hop in range(1, ns)), msg_s[0])
     for by in range(1, nx):
         gx_copy(by).start()
-    total = msg_x[0]
-    for by in range(1, nx):
-        gx_copy(by).wait_recv()
-        total = total + msg_x[by]
-    msg_z[z_at, 0:occs] = total
-    for k in range(pd):
-        for e in range(2):
-            msg_z[z_at, pl.ds(occs + 2 * k + e, 1)] = jnp.full((1, LANES), pairs[k, e], jnp.int32).astype(F32)
-    for by in range(1, nz):
-        gz_copy(by).start()
-
     for wave in range(waves):
         own = pl.ds(z_at * cg + wave * half, half)
         total = part[own]
@@ -269,6 +258,17 @@
         for by in range(1, nz):
             for copy in ag_copies(by, wave):
                 copy.start()
+        if wave == 0:
+            joined = msg_x[0]
+            for by in range(1, nx):
+                gx_copy(by).wait_recv()
+                joined = joined + msg_x[by]
+            msg_z[z_at, 0:occs] = joined
+            for k in range(pd):
+                for e in range(2):
+                    msg_z[z_at, pl.ds(occs + 2 * k + e, 1)] = jnp.full((1, LANES), pairs[k, e], jnp.int32).astype(F32)
+            for by in range(1, nz):
+                gz_copy(by).start()
 
     for by in range(1, nz):
         gz_copy(by).wait_recv()

time: 44.3 us -> 44.3 us (level)
  no operation moved by 1% of the time
where the time goes in v4:
time: 44.3 us; the launch traced here: 44.1 us
  Pallas kernels  39.1 us (88%)
  local copies, waits for them, and re-layouts  3.08 us (7%)
  other arithmetic  1.2 us (3%)
  between operations  0.66 us (1%)
    pallas_call x1, Pallas kernels, shards(): pl.pallas_call(functools.partial(kernel, dims), out_shape=(jax.ShapeDtype...  39.1 us
    unnamed x8, local copies, waits for them, and re-layouts  3 us
    mul x1, other arithmetic, shards(): virt = fin[:ng].astype(F32) * scale[:ng]  0.91 us

profile of v4, /device:TPU:0, one launch (start us, length us, event | category | flops | bytes accessed | tf_op | source)
XLA Modules:
  0.0 44.1 jit_solution(7156122484813001233)
XLA Ops:
  0.6 0.0 copy-start.2
  0.6 0.7 %copy-done.2 = s32[36,2]{0,1:T(2,128)S(1)} copy-done((s32[36,2]{0,1:T(2,128)S(1)}, s32[36,2]{0,1:T(2,128)}, u32[]{:S(2)}) %copy-start.2) | copy-done | bytes 312
  1.3 0.3 select_reduce_fusion
  1.6 0.1 add.8.table
  1.7 0.0 copy-start.1
  1.7 0.1 copy.6.tiles
  1.8 0.6 %copy-done.1 = s32[1,2]{1,0:T(1,128)S(1)} copy-done((s32[1,2]{1,0:T(1,128)S(1)}, s32[1,2]{1,0:T(1,128)}, u32[]{:S(2)}) %copy-start.1) | copy-done | bytes 32
  2.4 0.0 copy-start
  2.4 1.0 %copy-done = bf16[1,18,64,128]{3,2,1,0:T(8,128)(2,1)S(1)} copy-done((bf16[1,18,64,128]{3,2,1,0:T(8,128)(2,1)S(1)}, bf16[1,18,64,128]{3,2,1,0:T(8,128)(2,1)}, u32[]{:S(2)}) %copy-start) | copy-done | bytes 294936
  3.3 39.1 %shard_map.50 = (s16[72,16,128]{2,1,0:T(8,128)(2,1)S(1)}, f32[72,1,128]{2,1,0:T(1,128)S(1)}, f32[256,256]{1,0:T(8,128)S(1)}) custom-call(bf16[1,72,16,128]{3,2,1,0:T(8,128)(2,1)S(1)} %bitcast.7, s32[1,2]{1,0:T(1,128)S(1)} %copy-done.1, s32[36,2]{1,0:T(8,128)S(1)} %copy.6.tiles, s32[64]{0:T(128)S(1)} %add.8.table), custom_call_target="tpu_custom_call" | custom-call | tf_op jit(solution)/shard_map/pallas_call | solution.py:356
  42.5 0.9 %convert_multiply_fusion = f32[72,16,128]{2,1,0:T(8,128)} fusion(s16[72,16,128]{2,1,0:T(8,128)(2,1)S(1)} %get-tuple-element.5, f32[72,128]{1,0:T(8,128)S(1)} %bitcast.8), kind=kLoop, calls=%fused_computation | loop fusion | flops 294912 | bytes 921600 | tf_op jit(solution)/shard_map/mul | solution.py:385
  43.4 0.7 %copy.8 = f32[256,256]{1,0:T(8,128)} copy(f32[256,256]{1,0:T(8,128)S(1)} %get-tuple-element.15) | data formatting | bytes 524288
  (3 shorter events, 0.0 us)
Async XLA Ops:
  0.6 0.7 %copy-start.2 = (s32[36,2]{0,1:T(2,128)S(1)}, s32[36,2]{0,1:T(2,128)}, u32[]{:S(2)}) copy-start(s32[36,2]{0,1:T(2,128)} %param.5) | copy-start | bytes 868
  1.7 0.7 %copy-start.1 = (s32[1,2]{1,0:T(1,128)S(1)}, s32[1,2]{1,0:T(1,128)}, u32[]{:S(2)}) copy-start(s32[1,2]{1,0:T(1,128)} %pairs.1) | copy-start | bytes 28
  2.4 1.0 %copy-start = (bf16[1,18,64,128]{3,2,1,0:T(8,128)(2,1)S(1)}, bf16[1,18,64,128]{3,2,1,0:T(8,128)(2,1)}, u32[]{:S(2)}) copy-start(bf16[1,18,64,128]{3,2,1,0:T(8,128)(2,1)} %param.3) | copy-start | bytes 884740
